TPU v7x, 32 devices: a whole 2x2x4 slice. The times are simulated.
32 devices in a mesh: occ: 8 (over y, x, core), frag: 4 (over z).
Axes of the slice: x: 2, y: 2, z: 4, core: 2. Of those that a mesh axis runs over, the one named last changes fastest.
Arguments:
- factors: bfloat16 [32, 512, 1280], P(('frag', 'occ')), parts along dimension 0, may hold values from -1 to 1
- occ_energy: float32 [32], P('frag'), parts along dimension 0, may hold values from -2 to -0.3
- vir_energy: float32 [2048], P('frag'), parts along dimension 0, may hold values from 0.2 to 4
- coeffs: bfloat16 [4096, 512], P('frag'), parts along dimension 0, may hold values from -0.25 to 0.25
Outputs:
- back: bfloat16 [1280, 32, 1024], P('occ', 'frag'), parts along dimension 1
There are 4 independent parts, one for each index of `frag`. A program takes and returns all parts, laid end to end along the dimension named above; each array names one. Nothing has to cross between parts.
All inputs are finite; a program needn't handle non-finite values.
Results may differ from a plain program's by a relative error of at most 0.008.
Values may be sent and summed in bfloat16 or wider, within the bound.
A program may use at most 64 MiB of HBM per device.

v0:
```python
import jax
import jax.numpy as jnp
from jax import lax
from jax.sharding import PartitionSpec as P

OFFSETS = 3


def passed_along(block, axis, distance):
    devices = range(lax.axis_size(axis))
    route = [((i - distance) % len(devices), i) for i in devices]
    return lax.ppermute(block, axis, route)


def on_device(factors, occ_energy, vir_energy, coeffs):
    mine = factors[0]
    count = lax.axis_size("occ")
    index = lax.axis_index("occ")
    partners = []
    current = mine
    for offset in range(1, OFFSETS + 1):
        current = passed_along(current, "occ", -1)
        partners.append(current)
    own_energy = lax.dynamic_index_in_dim(occ_energy, index, 0, False)
    own = jnp.zeros((mine.shape[1], mine.shape[0]), jnp.float32)
    outgoing = []
    for offset in range(1, OFFSETS + 1):
        partner = partners[offset - 1]
        other_energy = lax.dynamic_index_in_dim(occ_energy, (index + offset) % count, 0, False)
        kmat = lax.dot_general(
            mine, partner, (((1,), (1,)), ((), ())), preferred_element_type=jnp.float32
        )
        denom = own_energy + other_energy - vir_energy[:, None] - vir_energy[None, :]
        amps = (kmat / denom).astype(jnp.bfloat16)
        own = own + lax.dot_general(
            partner, amps, (((0,), (1,)), ((), ())), preferred_element_type=jnp.float32
        )
        sent = lax.dot_general(
            mine, amps, (((0,), (0,)), ((), ())), preferred_element_type=jnp.float32
        )
        outgoing.append(sent.astype(jnp.bfloat16))
    incoming = jnp.zeros_like(own)
    for offset in range(1, OFFSETS + 1):
        arrived = passed_along(outgoing[offset - 1], "occ", offset)
        incoming = incoming + arrived.astype(jnp.float32)
    gamma = (own + incoming).astype(jnp.bfloat16)[None]
    slabs = lax.all_to_all(gamma, "occ", split_axis=1, concat_axis=0, tiled=True)
    return jnp.einsum("ipa,ma->pim", slabs, coeffs, preferred_element_type=jnp.float32).astype(
        jnp.bfloat16
    )


def solution(mesh):
    return jax.shard_map(
        on_device,
        mesh=mesh,
        in_specs=(P(("frag", "occ"), None, None), P("frag"), P("frag"), P("frag", None)),
        out_specs=P("occ", "frag", None),
        check_vma=False,
    )
```

profile of v0, /device:TPU:0, one launch (start us, length us, event | category | flops | bytes accessed | tf_op | source)
XLA Modules:
  0.0 173.1 jit_solution(9468343890820798394)
XLA Ops:
  0.0 3.4 %collective-permute-start = (bf16[512,1280]{1,0:T(8,128)(2,1)}, bf16[512,1280]{1,0:T(8,128)(2,1)}, u32[]{:S(2)}, u32[]{:S(2)}) collective-permute-start(bf16[512,1280]{1,0:T(8,128)(2,1)} %bitcast.56), channel_id=1, source_target_pairs={{4,0},{8,4},{12,8},{16,12},{20,16},{24,20},{28,24},{0,28},{5,1},{9... | collective-permute-start | bytes 3932168 | tf_op jit(solution)/shard_map/ppermute | solution.py:12
  3.4 15.4 %collective-permute-done = bf16[512,1280]{1,0:T(8,128)(2,1)} collective-permute-done((bf16[512,1280]{1,0:T(8,128)(2,1)}, bf16[512,1280]{1,0:T(8,128)(2,1)}, u32[]{:S(2)}, u32[]{:S(2)}) %collective-permute-start) | collective-permute-done | bytes 1310752 | tf_op jit(solution)/shard_map/ppermute | solution.py:12
  18.8 2.8 %collective-permute-start.1 = (bf16[512,1280]{1,0:T(8,128)(2,1)}, bf16[512,1280]{1,0:T(8,128)(2,1)S(1)}, u32[]{:S(2)}, u32[]{:S(2)}) collective-permute-start(bf16[512,1280]{1,0:T(8,128)(2,1)} %collective-permute-done), channel_id=1, source_target_pairs={{4,0},{8,4},{12,8},{16,12},{20,16},{24,20},{28,24},{0,28},{5,1},{9... | collective-permute-start | bytes 3932168 | tf_op jit(solution)/shard_map/ppermute | solution.py:12
  21.6 1.5 fusion.17
  26.8 0.7 broadcast_subtract_fusion
  27.5 9.5 %collective-permute-done.1 = bf16[512,1280]{1,0:T(8,128)(2,1)S(1)} collective-permute-done((bf16[512,1280]{1,0:T(8,128)(2,1)}, bf16[512,1280]{1,0:T(8,128)(2,1)S(1)}, u32[]{:S(2)}, u32[]{:S(2)}) %collective-permute-start.1) | collective-permute-done | bytes 1310752 | tf_op jit(solution)/shard_map/ppermute | solution.py:12
  37.1 2.7 %collective-permute-start.2 = (bf16[512,1280]{1,0:T(8,128)(2,1)S(1)}, bf16[512,1280]{1,0:T(8,128)(2,1)S(1)}, u32[]{:S(2)}, u32[]{:S(2)}) collective-permute-start(bf16[512,1280]{1,0:T(8,128)(2,1)S(1)} %collective-permute-done.1), channel_id=1, source_target_pairs={{4,0},{8,4},{12,8},{16,12},{20,16},{24,20},{28,24},{0,28},{5,1},{9... | collective-permute-start | bytes 3932168 | tf_op jit(solution)/shard_map/ppermute | solution.py:12
  39.8 2.7 %fusion.7 = bf16[512,512]{1,0:T(8,128)(2,1)S(1)} fusion(bf16[512,1280]{1,0:T(8,128)(2,1)} %collective-permute-done, f32[512]{0:T(512)} %param.6, f32[512]{0:T(512)S(1)} %get-tuple-element.6, bf16[1,512,1280]{2,1,0:T(8,128)(2,1)} %param.4), kind=kOutput, calls=%fused_computation.16 | convolution fusion | flops 671875072 | bytes 3149824 | tf_op jit(solution)/shard_map/dot_general | solution.py:30
  42.5 0.9 fusion.3
  43.4 0.1 collective-permute-start.3
  43.4 0.9 fusion.8
  44.3 0.9 fusion.4
  45.2 0.1 collective-permute-start.4
  45.3 22.8 %collective-permute-done.2 = bf16[512,1280]{1,0:T(8,128)(2,1)S(1)} collective-permute-done((bf16[512,1280]{1,0:T(8,128)(2,1)S(1)}, bf16[512,1280]{1,0:T(8,128)(2,1)S(1)}, u32[]{:S(2)}, u32[]{:S(2)}) %collective-permute-start.2) | collective-permute-done | bytes 1310752 | tf_op jit(solution)/shard_map/ppermute | solution.py:12
  68.0 0.9 fusion.9
  68.9 0.9 fusion.5
  69.8 0.9 collective-permute-start.5
  70.7 2.2 %fusion.18 = f32[512,1280]{1,0:T(8,128)S(1)} fusion(bf16[512,512]{1,0:T(8,128)(2,1)S(1)} %fusion.7, bf16[512,1280]{1,0:T(8,128)(2,1)} %collective-permute-done), kind=kOutput, calls=%fused_computation.30 | convolution fusion | flops 671088640 | bytes 4456448 | tf_op jit(solution)/shard_map/dot_general | solution.py:35
  72.8 0.8 convolution_add_fusion.1
  73.7 1.8 %collective-permute-done.3 = bf16[1280,512]{0,1:T(8,128)(2,1)S(1)} collective-permute-done((bf16[1280,512]{0,1:T(8,128)(2,1)S(1)}, bf16[1280,512]{0,1:T(8,128)(2,1)S(1)}, u32[]{:S(2)}, u32[]{:S(2)}) %collective-permute-start.3) | collective-permute-done | bytes 1310752 | tf_op jit(solution)/shard_map/ppermute | solution.py:12
  75.5 20.6 %collective-permute-done.4 = bf16[1280,512]{0,1:T(8,128)(2,1)S(1)} collective-permute-done((bf16[1280,512]{0,1:T(8,128)(2,1)S(1)}, bf16[1280,512]{0,1:T(8,128)(2,1)S(1)}, u32[]{:S(2)}, u32[]{:S(2)}) %collective-permute-start.4) | collective-permute-done | bytes 1310752 | tf_op jit(solution)/shard_map/ppermute | solution.py:12
  96.1 28.2 %collective-permute-done.5 = bf16[1280,512]{0,1:T(8,128)(2,1)S(1)} collective-permute-done((bf16[1280,512]{0,1:T(8,128)(2,1)S(1)}, bf16[1280,512]{0,1:T(8,128)(2,1)S(1)}, u32[]{:S(2)}, u32[]{:S(2)}) %collective-permute-start.5) | collective-permute-done | bytes 1310752 | tf_op jit(solution)/shard_map/ppermute | solution.py:12
  124.3 0.9 fusion.6
  125.3 4.1 %copy.9 = bf16[1,1280,512]{2,0,1:T(2,128)(2,1)} copy(bf16[1,1280,512]{1,2,0:T(8,128)(2,1)S(1)} %fusion.6) | data formatting | bytes 2621440 | tf_op jit(solution)/shard_map/broadcast_in_dim | solution.py:46
  129.3 0.6 broadcast.10
  129.9 9.5 %reduce = bf16[1280,512]{1,0:T(8,128)(2,1)S(1)} reduce(bf16[1280,1,512]{2,1,0:T(2,128)(2,1)} %bitcast.53, bf16[]{:T(256)} %broadcast.10), dimensions={1}, to_apply=%bitcast.38.reduce_sub_computation | reduce | bytes 2621442
  139.4 1.8 %reshape.14 = bf16[8,2,40960]{2,1,0:T(2,128)(2,1)} reshape(bf16[1280,512]{1,0:T(8,128)(2,1)S(1)} %reduce) | data formatting | bytes 2621440
  141.2 21.6 %all_to_all.12 = bf16[8,2,40960]{2,1,0:T(2,128)(2,1)S(1)} all-to-all(bf16[8,2,40960]{2,1,0:T(2,128)(2,1)} %reshape.14), channel_id=1, replica_groups=mesh['occ'=8,'frag'=4] {'occ'}, dimensions={0} | all-to-all | bytes 2621440 | tf_op jit(solution)/shard_map/all_to_all | solution.py:47
  162.8 3.6 %reshape.15 = bf16[1280,1,512]{2,1,0:T(2,128)(2,1)} reshape(bf16[8,2,40960]{2,1,0:T(2,128)(2,1)S(1)} %all_to_all.12) | data formatting | bytes 2621440
  166.5 2.1 %copy.11 = bf16[1,1280,512]{2,1,0:T(8,128)(2,1)S(1)} copy(bf16[1,1280,512]{2,0,1:T(2,128)(2,1)} %bitcast.54) | data formatting | bytes 2621440
  168.6 1.6 convert_bitcast_fusion
  170.2 2.9 %copy.10 = bf16[160,8,1024]{2,1,0:T(8,128)(2,1)} copy(bf16[160,8,1024]{2,0,1:T(8,128)(2,1)S(1)} %convert_bitcast_fusion) | data formatting | bytes 5242880 | tf_op jit(solution)/shard_map/convert_element_type | solution.py:48
  (6 shorter events, 0.0 us)
Async XLA Ops:
  0.0 168.6 %copy-start = (bf16[1024,512]{1,0:T(8,128)(2,1)S(1)}, bf16[1024,512]{1,0:T(8,128)(2,1)}, u32[]{:S(2)}) copy-start(bf16[1024,512]{1,0:T(8,128)(2,1)} %param.7) | copy-start | bytes 3145732
  0.0 18.8 %collective-permute-start = (bf16[512,1280]{1,0:T(8,128)(2,1)}, bf16[512,1280]{1,0:T(8,128)(2,1)}, u32[]{:S(2)}, u32[]{:S(2)}) collective-permute-start(bf16[512,1280]{1,0:T(8,128)(2,1)} %bitcast.56), channel_id=1, source_target_pairs={{4,0},{8,4},{12,8},{16,12},{20,16},{24,20},{28,24},{0,28},{5,1},{9... | collective-permute-start | bytes 3932168 | tf_op jit(solution)/shard_map/ppermute | solution.py:12
  18.8 18.2 %collective-permute-start.1 = (bf16[512,1280]{1,0:T(8,128)(2,1)}, bf16[512,1280]{1,0:T(8,128)(2,1)S(1)}, u32[]{:S(2)}, u32[]{:S(2)}) collective-permute-start(bf16[512,1280]{1,0:T(8,128)(2,1)} %collective-permute-done), channel_id=1, source_target_pairs={{4,0},{8,4},{12,8},{16,12},{20,16},{24,20},{28,24},{0,28},{5,1},{9... | collective-permute-start | bytes 3932168 | tf_op jit(solution)/shard_map/ppermute | solution.py:12
  37.1 31.0 %collective-permute-start.2 = (bf16[512,1280]{1,0:T(8,128)(2,1)S(1)}, bf16[512,1280]{1,0:T(8,128)(2,1)S(1)}, u32[]{:S(2)}, u32[]{:S(2)}) collective-permute-start(bf16[512,1280]{1,0:T(8,128)(2,1)S(1)} %collective-permute-done.1), channel_id=1, source_target_pairs={{4,0},{8,4},{12,8},{16,12},{20,16},{24,20},{28,24},{0,28},{5,1},{9... | collective-permute-start | bytes 3932168 | tf_op jit(solution)/shard_map/ppermute | solution.py:12
  39.8 2.7 %copy-start.2 = (bf16[1,512,1280]{2,1,0:T(8,128)(2,1)S(1)}, bf16[1,512,1280]{2,1,0:T(8,128)(2,1)}, u32[]{:S(2)}) copy-start(bf16[1,512,1280]{2,1,0:T(8,128)(2,1)} %param.4) | copy-start | bytes 3932164
  42.5 1.0 copy-start.1
  43.4 32.1 %collective-permute-start.3 = (bf16[1280,512]{0,1:T(8,128)(2,1)S(1)}, bf16[1280,512]{0,1:T(8,128)(2,1)S(1)}, u32[]{:S(2)}, u32[]{:S(2)}) collective-permute-start(bf16[1280,512]{0,1:T(8,128)(2,1)S(1)} %fusion.3), channel_id=1, source_target_pairs={{28,0},{0,4},{4,8},{8,12},{12,16},{16,20},{20,24},{24,28},{29,1},{... | collective-permute-start | bytes 3932168 | tf_op jit(solution)/shard_map/ppermute | solution.py:12
  45.2 50.9 %collective-permute-start.4 = (bf16[1280,512]{0,1:T(8,128)(2,1)S(1)}, bf16[1280,512]{0,1:T(8,128)(2,1)S(1)}, u32[]{:S(2)}, u32[]{:S(2)}) collective-permute-start(bf16[1280,512]{0,1:T(8,128)(2,1)S(1)} %fusion.4), channel_id=1, source_target_pairs={{24,0},{28,4},{0,8},{4,12},{8,16},{12,20},{16,24},{20,28},{25,1},{... | collective-permute-start | bytes 3932168 | tf_op jit(solution)/shard_map/ppermute | solution.py:12
  69.8 54.5 %collective-permute-start.5 = (bf16[1280,512]{0,1:T(8,128)(2,1)S(1)}, bf16[1280,512]{0,1:T(8,128)(2,1)S(1)}, u32[]{:S(2)}, u32[]{:S(2)}) collective-permute-start(bf16[1280,512]{0,1:T(8,128)(2,1)S(1)} %fusion.5), channel_id=1, source_target_pairs={{20,0},{24,4},{28,8},{0,12},{4,16},{8,20},{12,24},{16,28},{21,1},{... | collective-permute-start | bytes 3932168 | tf_op jit(solution)/shard_map/ppermute | solution.py:12
where the time goes:
time: 173 us
  waiting for transfers between devices  98.4 us (57%)
  blocking collectives  21.6 us (12%)
  local copies, waits for them, and re-layouts  16.6 us (10%)
  matrix products  12.6 us (7%)
  other arithmetic  10.2 us (6%)
  starting transfers between devices  9.87 us (6%)
  between operations  3.89 us (2%)
    ppermute x6, waiting for transfers between devices, passed_along(): return lax.ppermute(block, axis, route)  98.4 us
    all_to_all x1, blocking collectives, on_device(): lax.all_to_all(gamma, 'occ', split_axis=1, concat_axis=0, tiled=True)  21.6 us
    ppermute x6, starting transfers between devices, passed_along(): return lax.ppermute(block, axis, route)  9.87 us
    unnamed x1, other arithmetic  9.47 us
    unnamed x10, local copies, waits for them, and re-layouts  8.17 us
    dot_general x3, matrix products, on_device(): lax.dot_general(mine, partner, (((1,), (1,)), ((), ())), preferred_elemen...  4.45 us
    broadcast_in_dim x1, local copies, waits for them, and re-layouts, on_device(): gamma = (own + incoming).astype(jnp.bfloat16)[None]  4.07 us
    dot_general x3, matrix products, on_device(): lax.dot_general(partner, amps, (((0,), (1,)), ((), ())), preferred_elemen...  3.94 us
  transfers between devices with their start and end apart: 6, of which 6 were waited for; matrix products, arithmetic and copies ran while one was open for 7% of the time, Pallas kernels for 0%

commit v1 on v0

--- a/solution.py
+++ b/solution.py
@@ -44,7 +44,10 @@
         arrived = passed_along(outgoing[offset - 1], "occ", offset)
         incoming = incoming + arrived.astype(jnp.float32)
     gamma = (own + incoming).astype(jnp.bfloat16)[None]
-    slabs = lax.all_to_all(gamma, "occ", split_axis=1, concat_axis=0, tiled=True)
+    slabs = jnp.concatenate(
+        lax.all_to_all(jnp.stack(jnp.split(gamma, lax.axis_size("occ"), axis=1)), "occ", 0, 0),
+        axis=0,
+    )
     return jnp.einsum("ipa,ma->pim", slabs, coeffs, preferred_element_type=jnp.float32).astype(
         jnp.bfloat16
     )

time: 173 us -> 160 us (0.925)
  other arithmetic: 10.2 us -> 0.69 us
  local copies, waits for them, and re-layouts: 16.6 us -> 13.8 us
    unnamed x1 -> x0, other arithmetic: 9.47 us -> none
    broadcast_in_dim x1 -> x0, local copies, waits for them, and re-layouts: 4.07 us -> none  [on_device(): gamma = (own + incoming).astype(jnp.bfloat16)[None]]
    another operation x0 -> x2, local copies, waits for them, and re-layouts: none -> 3.79 us  [on_device(): jnp.stack(jnp.split(gamma, lax.axis_size('occ'), axis=1))]
    unnamed x10 -> x13, local copies, waits for them, and re-layouts: 8.17 us -> 5.67 us
  transfers between devices with their start and end apart: 6 -> 6, of which waited for: 6 -> 6; matrix products, arithmetic and copies ran while one was open for 7% -> 8% of each run, Pallas kernels for 0% -> 0%
where the time goes in v1:
time: 160 us
  waiting for transfers between devices  98.4 us (62%)
  blocking collectives  20.6 us (13%)
  local copies, waits for them, and re-layouts  13.8 us (9%)
  matrix products  12.6 us (8%)
  starting transfers between devices  9.87 us (6%)
  between operations  3.81 us (2%)
    ppermute x6, waiting for transfers between devices, passed_along(): return lax.ppermute(block, axis, route)  98.4 us
    all_to_all x1, blocking collectives, on_device(): lax.all_to_all(jnp.stack(jnp.split(gamma, lax.axis_size('occ'), axis=1)),...  20.6 us
    ppermute x6, starting transfers between devices, passed_along(): return lax.ppermute(block, axis, route)  9.87 us
    unnamed x13, local copies, waits for them, and re-layouts  5.67 us
    dot_general x3, matrix products, on_device(): lax.dot_general(mine, partner, (((1,), (1,)), ((), ())), preferred_elemen...  4.45 us
    dot_general x3, matrix products, on_device(): lax.dot_general(partner, amps, (((0,), (1,)), ((), ())), preferred_elemen...  3.94 us
    another operation x2, local copies, waits for them, and re-layouts, on_device(): jnp.stack(jnp.split(gamma, lax.axis_size('occ'), axis=1))  3.79 us
  transfers between devices with their start and end apart: 6, of which 6 were waited for; matrix products, arithmetic and copies ran while one was open for 8% of the time, Pallas kernels for 0%

profile of v1, /device:TPU:0, one launch (start us, length us, event | category | flops | bytes accessed | tf_op | source)
XLA Modules:
  0.0 159.8 jit_solution(658077072128021899)
XLA Ops:
  0.0 3.4 %collective-permute-start = (bf16[512,1280]{1,0:T(8,128)(2,1)}, bf16[512,1280]{1,0:T(8,128)(2,1)}, u32[]{:S(2)}, u32[]{:S(2)}) collective-permute-start(bf16[512,1280]{1,0:T(8,128)(2,1)} %bitcast.84), channel_id=1, source_target_pairs={{4,0},{8,4},{12,8},{16,12},{20,16},{24,20},{28,24},{0,28},{5,1},{9... | collective-permute-start | bytes 3932168 | tf_op jit(solution)/shard_map/ppermute | solution.py:12
  3.4 15.4 %collective-permute-done = bf16[512,1280]{1,0:T(8,128)(2,1)} collective-permute-done((bf16[512,1280]{1,0:T(8,128)(2,1)}, bf16[512,1280]{1,0:T(8,128)(2,1)}, u32[]{:S(2)}, u32[]{:S(2)}) %collective-permute-start) | collective-permute-done | bytes 1310752 | tf_op jit(solution)/shard_map/ppermute | solution.py:12
  18.8 2.8 %collective-permute-start.1 = (bf16[512,1280]{1,0:T(8,128)(2,1)}, bf16[512,1280]{1,0:T(8,128)(2,1)S(1)}, u32[]{:S(2)}, u32[]{:S(2)}) collective-permute-start(bf16[512,1280]{1,0:T(8,128)(2,1)} %collective-permute-done), channel_id=1, source_target_pairs={{4,0},{8,4},{12,8},{16,12},{20,16},{24,20},{28,24},{0,28},{5,1},{9... | collective-permute-start | bytes 3932168 | tf_op jit(solution)/shard_map/ppermute | solution.py:12
  21.6 1.5 fusion.26
  27.5 9.6 %collective-permute-done.1 = bf16[512,1280]{1,0:T(8,128)(2,1)S(1)} collective-permute-done((bf16[512,1280]{1,0:T(8,128)(2,1)}, bf16[512,1280]{1,0:T(8,128)(2,1)S(1)}, u32[]{:S(2)}, u32[]{:S(2)}) %collective-permute-start.1) | collective-permute-done | bytes 1310752 | tf_op jit(solution)/shard_map/ppermute | solution.py:12
  37.1 2.7 %collective-permute-start.2 = (bf16[512,1280]{1,0:T(8,128)(2,1)S(1)}, bf16[512,1280]{1,0:T(8,128)(2,1)S(1)}, u32[]{:S(2)}, u32[]{:S(2)}) collective-permute-start(bf16[512,1280]{1,0:T(8,128)(2,1)S(1)} %collective-permute-done.1), channel_id=1, source_target_pairs={{4,0},{8,4},{12,8},{16,12},{20,16},{24,20},{28,24},{0,28},{5,1},{9... | collective-permute-start | bytes 3932168 | tf_op jit(solution)/shard_map/ppermute | solution.py:12
  39.8 2.7 %fusion.8 = bf16[512,512]{1,0:T(8,128)(2,1)S(1)} fusion(bf16[512,1280]{1,0:T(8,128)(2,1)} %collective-permute-done, f32[512]{0:T(512)} %param.6, f32[512]{0:T(512)S(1)} %get-tuple-element.6, bf16[1,512,1280]{2,1,0:T(8,128)(2,1)} %param.4), kind=kOutput, calls=%fused_computation.17 | convolution fusion | flops 671875072 | bytes 3149824 | tf_op jit(solution)/shard_map/dot_general | solution.py:30
  42.5 0.9 fusion.3
  43.4 0.9 fusion.9
  44.3 0.9 fusion.4
  45.3 22.8 %collective-permute-done.2 = bf16[512,1280]{1,0:T(8,128)(2,1)S(1)} collective-permute-done((bf16[512,1280]{1,0:T(8,128)(2,1)S(1)}, bf16[512,1280]{1,0:T(8,128)(2,1)S(1)}, u32[]{:S(2)}, u32[]{:S(2)}) %collective-permute-start.2) | collective-permute-done | bytes 1310752 | tf_op jit(solution)/shard_map/ppermute | solution.py:12
  68.0 0.9 fusion.10
  68.9 0.9 fusion.5
  69.8 0.9 collective-permute-start.5
  70.7 2.2 %fusion.27 = f32[512,1280]{1,0:T(8,128)S(1)} fusion(bf16[512,512]{1,0:T(8,128)(2,1)S(1)} %fusion.8, bf16[512,1280]{1,0:T(8,128)(2,1)} %collective-permute-done), kind=kOutput, calls=%fused_computation.47 | convolution fusion | flops 671088640 | bytes 4456448 | tf_op jit(solution)/shard_map/dot_general | solution.py:35
  72.8 0.8 convolution_add_fusion.1
  73.7 1.8 %collective-permute-done.3 = bf16[1280,512]{0,1:T(8,128)(2,1)S(1)} collective-permute-done((bf16[1280,512]{0,1:T(8,128)(2,1)S(1)}, bf16[1280,512]{0,1:T(8,128)(2,1)S(1)}, u32[]{:S(2)}, u32[]{:S(2)}) %collective-permute-start.3) | collective-permute-done | bytes 1310752 | tf_op jit(solution)/shard_map/ppermute | solution.py:12
  75.5 20.6 %collective-permute-done.4 = bf16[1280,512]{0,1:T(8,128)(2,1)S(1)} collective-permute-done((bf16[1280,512]{0,1:T(8,128)(2,1)S(1)}, bf16[1280,512]{0,1:T(8,128)(2,1)S(1)}, u32[]{:S(2)}, u32[]{:S(2)}) %collective-permute-start.4) | collective-permute-done | bytes 1310752 | tf_op jit(solution)/shard_map/ppermute | solution.py:12
  96.1 28.2 %collective-permute-done.5 = bf16[1280,512]{0,1:T(8,128)(2,1)S(1)} collective-permute-done((bf16[1280,512]{0,1:T(8,128)(2,1)S(1)}, bf16[1280,512]{0,1:T(8,128)(2,1)S(1)}, u32[]{:S(2)}, u32[]{:S(2)}) %collective-permute-start.5) | collective-permute-done | bytes 1310752 | tf_op jit(solution)/shard_map/ppermute | solution.py:12
  124.3 0.9 fusion.6
  125.3 0.7 fusion.19
  126.0 0.8 fusion.18
  126.8 0.8 fusion.17
  127.7 0.8 fusion.16
  128.5 0.7 fusion.15
  129.2 0.8 fusion.14
  130.1 0.8 fusion.13
  130.9 0.8 fusion.12
  131.8 2.9 %copy.7 = bf16[8,1,160,512]{3,2,1,0:T(8,128)(2,1)S(1)} copy(bf16[8,1,160,512]{2,3,1,0:T(8,128)(2,1)} %fusion.12) | data formatting | bytes 2621440 | tf_op jit(solution)/shard_map/stack | solution.py:48
  134.7 20.6 %all_to_all.5 = bf16[8,1,160,512]{3,2,1,0:T(8,128)(2,1)S(1)} all-to-all(bf16[8,1,160,512]{3,2,1,0:T(8,128)(2,1)S(1)} %copy.7), channel_id=1, replica_groups=mesh['occ'=8,'frag'=4] {'occ'}, dimensions={0} | all-to-all | bytes 2621440 | tf_op jit(solution)/shard_map/all_to_all | solution.py:48
  155.3 1.6 convert_bitcast_fusion
  156.9 2.9 %copy.8 = bf16[160,8,1024]{2,1,0:T(8,128)(2,1)} copy(bf16[160,8,1024]{2,0,1:T(8,128)(2,1)S(1)} %convert_bitcast_fusion) | data formatting | bytes 5242880 | tf_op jit(solution)/shard_map/convert_element_type | solution.py:51
  (9 shorter events, 0.8 us)
Async XLA Ops:
  0.0 155.3 %copy-start = (bf16[1024,512]{1,0:T(8,128)(2,1)S(1)}, bf16[1024,512]{1,0:T(8,128)(2,1)}, u32[]{:S(2)}) copy-start(bf16[1024,512]{1,0:T(8,128)(2,1)} %param.7) | copy-start | bytes 3145732
  0.0 18.8 %collective-permute-start = (bf16[512,1280]{1,0:T(8,128)(2,1)}, bf16[512,1280]{1,0:T(8,128)(2,1)}, u32[]{:S(2)}, u32[]{:S(2)}) collective-permute-start(bf16[512,1280]{1,0:T(8,128)(2,1)} %bitcast.84), channel_id=1, source_target_pairs={{4,0},{8,4},{12,8},{16,12},{20,16},{24,20},{28,24},{0,28},{5,1},{9... | collective-permute-start | bytes 3932168 | tf_op jit(solution)/shard_map/ppermute | solution.py:12
  18.8 18.2 %collective-permute-start.1 = (bf16[512,1280]{1,0:T(8,128)(2,1)}, bf16[512,1280]{1,0:T(8,128)(2,1)S(1)}, u32[]{:S(2)}, u32[]{:S(2)}) collective-permute-start(bf16[512,1280]{1,0:T(8,128)(2,1)} %collective-permute-done), channel_id=1, source_target_pairs={{4,0},{8,4},{12,8},{16,12},{20,16},{24,20},{28,24},{0,28},{5,1},{9... | collective-permute-start | bytes 3932168 | tf_op jit(solution)/shard_map/ppermute | solution.py:12
  37.1 31.0 %collective-permute-start.2 = (bf16[512,1280]{1,0:T(8,128)(2,1)S(1)}, bf16[512,1280]{1,0:T(8,128)(2,1)S(1)}, u32[]{:S(2)}, u32[]{:S(2)}) collective-permute-start(bf16[512,1280]{1,0:T(8,128)(2,1)S(1)} %collective-permute-done.1), channel_id=1, source_target_pairs={{4,0},{8,4},{12,8},{16,12},{20,16},{24,20},{28,24},{0,28},{5,1},{9... | collective-permute-start | bytes 3932168 | tf_op jit(solution)/shard_map/ppermute | solution.py:12
  39.8 2.7 %copy-start.2 = (bf16[1,512,1280]{2,1,0:T(8,128)(2,1)S(1)}, bf16[1,512,1280]{2,1,0:T(8,128)(2,1)}, u32[]{:S(2)}) copy-start(bf16[1,512,1280]{2,1,0:T(8,128)(2,1)} %param.4) | copy-start | bytes 3932164
  42.5 1.0 copy-start.1
  43.4 32.1 %collective-permute-start.3 = (bf16[1280,512]{0,1:T(8,128)(2,1)S(1)}, bf16[1280,512]{0,1:T(8,128)(2,1)S(1)}, u32[]{:S(2)}, u32[]{:S(2)}) collective-permute-start(bf16[1280,512]{0,1:T(8,128)(2,1)S(1)} %fusion.3), channel_id=1, source_target_pairs={{28,0},{0,4},{4,8},{8,12},{12,16},{16,20},{20,24},{24,28},{29,1},{... | collective-permute-start | bytes 3932168 | tf_op jit(solution)/shard_map/ppermute | solution.py:12
  45.2 50.9 %collective-permute-start.4 = (bf16[1280,512]{0,1:T(8,128)(2,1)S(1)}, bf16[1280,512]{0,1:T(8,128)(2,1)S(1)}, u32[]{:S(2)}, u32[]{:S(2)}) collective-permute-start(bf16[1280,512]{0,1:T(8,128)(2,1)S(1)} %fusion.4), channel_id=1, source_target_pairs={{24,0},{28,4},{0,8},{4,12},{8,16},{12,20},{16,24},{20,28},{25,1},{... | collective-permute-start | bytes 3932168 | tf_op jit(solution)/shard_map/ppermute | solution.py:12
  69.8 54.5 %collective-permute-start.5 = (bf16[1280,512]{0,1:T(8,128)(2,1)S(1)}, bf16[1280,512]{0,1:T(8,128)(2,1)S(1)}, u32[]{:S(2)}, u32[]{:S(2)}) collective-permute-start(bf16[1280,512]{0,1:T(8,128)(2,1)S(1)} %fusion.5), channel_id=1, source_target_pairs={{20,0},{24,4},{28,8},{0,12},{4,16},{8,20},{12,24},{16,28},{21,1},{... | collective-permute-start | bytes 3932168 | tf_op jit(solution)/shard_map/ppermute | solution.py:12
